TPU v7x, 256 devices: a whole 4x4x8 slice. The times are simulated.
256 devices in a mesh: row: 16 (over z, core), col: 16 (over y, x).
Axes of the slice: x: 4, y: 4, z: 8, core: 2. Of those that a mesh axis runs over, the one named last changes fastest.
Arguments:
- design: float32 [8192, 65536], P('row', 'col'), may hold values from -0.0625 to 0.0625
- targets: float32 [32, 8192], P(None, 'row'), may hold values from -6 to 6
- warm_solution: float32 [32, 65536], P(None, ('col', 'row')), may hold values from -2 to 2
- warm_sparse: float32 [32, 65536], P(None, ('col', 'row')), may hold values from -2 to 2
- warm_dual: float32 [32, 65536], P(None, ('col', 'row')), may hold values from -1.5 to 1.5
- sparsity: float32 [32], replicated, may hold values from 0.02 to 0.2
Outputs:
- solution: float32 [32, 65536], P(None, ('col', 'row'))
- sparse: float32 [32, 65536], P(None, ('col', 'row'))
- scaled_dual: float32 [32, 65536], P(None, ('col', 'row'))
All inputs are finite; a program needn't handle non-finite values.
Results may differ from a plain program's by a relative error of at most 0.0003.
Values sent between devices are 32-bit elements; how exact they have to be, the bound alone decides.
No kernel may reach another device: no remote copies, remote signals or barrier semaphores. Data moves between devices by JAX's collectives and lax.ppermute only.
A program may use at most 64 MiB of HBM per device.

v0:
```python
import jax
import jax.numpy as jnp
from jax import lax
from jax.experimental import pallas as pl
from jax.experimental.pallas import tpu as pltpu
from jax.sharding import Mesh
from jax.sharding import PartitionSpec as P


STEPS = 3
COL = ("col_0", "col_1")
ROW = ("row_0", "row_1")
COL_ROW = ("col_0", "col_1", "row_0", "row_1")

penalty = 0.5
Z = 8
K = 32
W = 512
H = 256
S = 128
T = 4 * K + 8


def pair(x):
    return lax.ppermute(x, "row_1", [(0, 1), (1, 0)])


def along_z(x, k):
    table = []
    for z in range(Z):
        table.append((2 * z, 2 * ((z + k) % Z)))
        table.append((2 * z + 1, 2 * ((z - k) % Z) + 1))
    return lax.ppermute(x, ROW, table)


def ring_parts(x, axis):
    n = 4
    parts = [x]
    for k in (2, 1, 3):
        parts.append(lax.ppermute(x, axis, [(i, (i + k) % n) for i in range(n)]))
    return parts


def split(x):
    hi = x.astype(jnp.bfloat16)
    return hi, (x - hi.astype(jnp.float32)).astype(jnp.bfloat16)


def dot(a, b, transposed):
    dims = (((1,), (1 if transposed else 0,)), ((), ()))
    return lax.dot_general(a, b, dims, preferred_element_type=jnp.float32)


def product(both, hi, lo, transposed):
    wide = dot(both, hi, transposed)
    return (wide[:K] + wide[K:]) + dot(both[:K], lo, transposed)


def columns(place, offset):
    at = lax.rem(place[0] + place[1] * offset + 2 * Z, Z)
    return pl.ds(pl.multiple_of(at * W, W), W)


def lanes(*stats):
    lane = lax.broadcasted_iota(jnp.int32, (K, S), 1)
    out = jnp.zeros((K, S), jnp.float32)
    for i, stat in enumerate(stats):
        out = jnp.where(lane == i, stat, out)
    return out


def flipped(stats):
    return jnp.transpose(jnp.concatenate([stats, jnp.zeros((S - K, S), jnp.float32)], 0))[:8]


def restored(tile):
    return jnp.transpose(jnp.concatenate([tile, jnp.zeros((S - 8, S), jnp.float32)], 0))[:K]


def row_sums(values):
    return jnp.sum(values, axis=1, keepdims=True)


def forward_offset(j):
    return Z - j


def forward_kernel(
    place, hi, lo, chip, mine, theirs, state, part, before, direction, found,
    out, after, found_out, both, acc, top,
):
    early = place[3] < 2
    total = mine[3 * T + 2 * K :]
    for i in range(3):
        at = slice(i * T + 4 * K, (i + 1) * T)
        total = total + (mine[at] + theirs[at])
    total = part[...] + restored(total)
    alpha = state[:, 0:1] / (total[:, 0:1] + penalty * state[:, 1:2])
    alpha = jnp.where(early, -1.0, alpha)
    kept = jnp.where(early, 0.0, 1.0)
    found_out[...] = found[...] + alpha * direction[0]
    first = place[2] == 0
    R = 16
    tops = []

    def piece(ref, index, count, i):
        starts = [index * T + c * K + i * R for c in range(count)]
        return jnp.concatenate([ref[at : at + R] for at in starts], 1)

    for i in range(K // R):
        rows = pl.ds(i * R, R)
        squares = crossed = None
        for j in range(Z):
            if j == 0:
                value = chip[rows, :]
            elif j < 4:
                value = piece(mine, j - 1, 4, i)
            elif j > 4:
                value = piece(theirs, 7 - j, 4, i)
            else:
                a, b = piece(mine, 3, 2, i), piece(theirs, 3, 2, i)
                value = jnp.concatenate([jnp.where(first, a, b), jnp.where(first, b, a)], 1)
            old = direction[j, rows, :]
            value = kept * before[j, rows, :] - alpha[i * R : i * R + R] * (value + penalty * old)
            after[j, rows, :] = value
            squares = value * value if squares is None else squares + value * value
            crossed = value * old if crossed is None else crossed + value * old
            big, small = split(value)
            at = columns(place, forward_offset(j))
            both[rows, at] = big
            both[pl.ds(K + i * R, R), at] = small
        tops.append([row_sums(squares), row_sums(crossed)])
    acc[:, : 2 * K] = dot(hi[...], both[...], True)
    acc[:, 2 * K : 3 * K] = dot(lo[...], both[:K], True)
    top[...] = jnp.transpose(acc[...])
    value = (top[:K] + top[K : 2 * K]) + top[2 * K : 3 * K]
    for c in range(4):
        out[c * K : (c + 1) * K] = value[:, c * S : (c + 1) * S]
    out[4 * K :] = flipped(lanes(*[jnp.concatenate(list(pieces), 0) for pieces in zip(*tops)]))


def chunks(place, hi, lo, values, side, which, out):
    both = jnp.concatenate(split(values), 0)
    for i in range(3):
        at = columns(place, side * (i + 1))
        out[:, i * W : (i + 1) * W] = product(both, hi[:, at], lo[:, at], False)
    for i in range(2):
        start = lax.rem(place[0] + Z // 2 * (1 - i), Z) * W + which * H
        at = pl.ds(pl.multiple_of(start, H), H)
        spot = 3 * W + i * H
        out[:, spot : spot + H] = product(both, hi[:, at], lo[:, at], False)
    out[:, 4 * W :] = lanes(row_sums(values * values))


def send_kernel(place, hi, lo, a, b, c, d, state, image, send, image_out, state_out):
    turn = place[3]
    payload = (a[...] + b[...]) + (c[...] + d[...])
    stats = restored(payload[4 * K :])
    payload = jnp.concatenate([payload[c * K : (c + 1) * K] for c in range(4)], 1)
    norm = stats[:, 0:1]
    ratio = norm / state[:, 0:1]
    ratio = jnp.where(turn == 0, 1.0, jnp.where(turn == 1, 0.0, ratio))
    square = norm + ratio * (2.0 * stats[:, 1:2] + ratio * state[:, 1:2])
    values = jnp.where(turn == 0, -1.0, 1.0) * payload + ratio * image[...]
    image_out[...] = values
    state_out[...] = lanes(norm, square, ratio)
    chunks(place, hi, lo, values, -1, 1 - place[2], send)


def keep_kernel(place, hi, lo, state, image, after, direction, keep, direction_out):
    fresh = jnp.where(place[3] == 0, 0.0, 1.0)
    ratio = state[:, 2:3]
    for j in range(Z):
        direction_out[j] = fresh * after[j] + ratio * direction[j]
    chunks(place, hi, lo, image[...], 1, place[2], keep)


VMEM = pl.BlockSpec(memory_space=pltpu.VMEM)
SMEM = pl.BlockSpec(memory_space=pltpu.SMEM)
ANY = pl.BlockSpec(memory_space=pl.ANY)


def array(*shape):
    return jax.ShapeDtypeStruct(shape, jnp.float32)


def call(kernel, kinds, outs, scratch, limit, *args, flops=10**9):
    return pl.pallas_call(
        kernel,
        in_specs=kinds + [VMEM] * (len(args) - len(kinds)),
        out_specs=[VMEM] * len(outs),
        out_shape=outs,
        scratch_shapes=scratch,
        cost_estimate=pl.CostEstimate(flops=flops, transcendentals=0, bytes_accessed=2**23),
        compiler_params=pltpu.CompilerParams(vmem_limit_bytes=limit * 2**20),
    )(*args)


STACK = array(Z, K, W)
TERM = jax.ShapeDtypeStruct((W, Z * W), jnp.bfloat16)
WIDE = array(K, 4 * W + S)


def prepare_kernel(design, hi, lo):
    for i in range(0, W, 64):
        hi[i : i + 64], lo[i : i + 64] = split(design[i : i + 64])


def prepare(design):
    block = pl.BlockSpec((W, 2 * W), lambda j: (0, j))
    return pl.pallas_call(
        prepare_kernel,
        grid=(Z // 2,),
        in_specs=[block],
        out_specs=[block, block],
        out_shape=[TERM, TERM],
        cost_estimate=pl.CostEstimate(flops=10**10, transcendentals=0, bytes_accessed=2**24),
        compiler_params=pltpu.CompilerParams(vmem_limit_bytes=58 * 2**20),
    )(design)


def pack_kernel(place, chip, extra, whole, small):
    tile = flipped(extra[...])
    for c in range(4):
        whole[c * K : (c + 1) * K] = chip[:, c * S : (c + 1) * S]
    whole[4 * K :] = tile
    for c in range(2):
        one, two = chip[:, c * S : (c + 1) * S], chip[:, H + c * S : H + (c + 1) * S]
        small[c * K : (c + 1) * K] = jnp.where(place[2] == 0, one, two)
    small[2 * K :] = tile


def forward(*args):
    scratch = [
        pltpu.VMEM((2 * K, Z * W), jnp.bfloat16),
        pltpu.VMEM((W, 4 * K), jnp.float32),
        pltpu.VMEM((4 * K, W), jnp.float32),
    ]
    return call(forward_kernel, [SMEM], [array(T, S), STACK, array(K, W)], scratch, 24, *args)


def on_device(design, targets, warm_solution, warm_sparse, warm_dual, sparsity):
    z = lax.axis_index("row_0")
    core = lax.axis_index("row_1")

    def place(turn):
        return jnp.stack([z, 1 - 2 * core, core, turn]).astype(jnp.int32)

    def half(x):
        return jnp.where(core == 0, x[:, :H], x[:, H : 2 * H])

    def joined(mine, other):
        return jnp.where(core == 0, jnp.concatenate([mine, other], 1), jnp.concatenate([other, mine], 1))

    def gathered(at, chip, extra):
        outs = [array(T, S), array(2 * K + 8, S)]
        whole, small = call(pack_kernel, [SMEM], outs, [], 24, at, chip, extra, flops=10**11)
        parts = {}
        for k in (4, 3, 2, 1):
            parts[k] = along_z(small if k == 4 else whole, k)
        mine = jnp.concatenate([parts[k] for k in (1, 2, 3, 4)], 0)
        return mine, pair(mine)

    def reduced(both):
        got4 = along_z(both[:, 3 * W : 3 * W + H], 4)
        got3 = along_z(both[:, 2 * W : 3 * W], 3)
        got2 = along_z(both[:, W : 2 * W], 2)
        got1 = along_z(both[:, :W], 1)
        mine = got4 + both[:, 3 * W + H : 4 * W]
        side = (got1 + got2 + got3) + joined(mine, jnp.zeros_like(mine))
        return side + pair(side), both[:, 4 * W :]

    def plane(x):
        a, b, c, d = ring_parts(x, "col_1")
        return ring_parts((a + b) + (c + d), "col_0")

    found = joined(warm_solution, pair(warm_solution))
    shift = penalty * (warm_sparse - warm_dual - warm_solution)
    shift = joined(shift, pair(shift))
    none = jnp.zeros((K, S), jnp.float32)
    stack = jnp.zeros((Z, K, W), jnp.float32)

    hi, lo = prepare(design)

    def ahead(turn, carry):
        chip, part, state, residual, direction, found, _ = carry
        at = place(turn)
        mine, theirs = gathered(at, chip, part)
        value, residual, found = forward(
            at, hi, lo, chip, mine, theirs, state, part, residual, direction, found
        )
        return at, plane(value), residual, found

    def advance(turn, carry):
        at, parts, residual, found = ahead(turn, carry)
        state, direction, image = carry[2], carry[4], carry[6]
        outs = [WIDE, array(K, W), array(K, S)]
        send, image, state = call(send_kernel, [SMEM], outs, [], 24, at, hi, lo, *parts, state, image)
        theirs = pair(send)
        keep, direction = call(
            keep_kernel, [SMEM], [WIDE, STACK], [], 24, at, hi, lo, state, image, residual, direction
        )
        chip, part = reduced(keep + theirs)
        chip = chip + jnp.where(turn == 0, shift, 0.0)
        return chip, part, state, residual, direction, found, image

    carry = lax.fori_loop(0, STEPS, advance, (found, none, none, stack, stack, found, targets))
    state, direction, image = carry[2], carry[4], carry[6]
    _, parts, residual, found = ahead(STEPS, carry)
    payload = (parts[0] + parts[1]) + (parts[2] + parts[3])
    stats = jnp.transpose(payload[4 * K :, :K])
    norm = stats[:, 0:1]
    ratio = norm / state[:, 0:1]
    square = norm + ratio * (2.0 * stats[:, 1:2] + ratio * state[:, 1:2])
    image = jnp.concatenate([payload[c * K : (c + 1) * K] for c in range(4)], 1) + ratio * image
    direction = half(residual[0]) + ratio * half(direction[0])
    part = jnp.pad(row_sums(image * image)[:, 0], (0, S - K))
    sent = lax.all_to_all(jnp.broadcast_to(part, (16, 8, S)), ROW, 0, 0, tiled=True)
    part = jnp.sum(sent, axis=0)[0, :K, None]
    solution = half(found) + norm / (part + penalty * square) * direction

    thresh = (sparsity / penalty)[:, None]
    merged = solution + warm_dual
    sparse = jnp.sign(merged) * jnp.maximum(jnp.abs(merged) - thresh, 0.0)
    return solution, sparse, merged - sparse


def solution(mesh):
    finer = Mesh(mesh.devices.reshape(8, 2, 4, 4), ("row_0", "row_1", "col_0", "col_1"))

    return jax.shard_map(
        on_device,
        mesh=finer,
        in_specs=(
            P(ROW, COL),
            P(None, ROW),
            P(None, COL_ROW),
            P(None, COL_ROW),
            P(None, COL_ROW),
            P(),
        ),
        out_specs=(P(None, COL_ROW), P(None, COL_ROW), P(None, COL_ROW)),
        check_vma=False,
    )
```

profile of v0, /device:TPU:2, one launch (start us, length us, event | category | flops | bytes accessed | tf_op | source)
XLA Modules:
  0.0 224.7 jit_solution(4957567166752439059)
XLA Ops:
  2.1 7.5 %shard_map.85 = (bf16[512,4096]{1,0:T(8,128)(2,1)}, bf16[512,4096]{1,0:T(8,128)(2,1)}) custom-call(f32[512,4096]{1,0:T(8,128)} %design.1), custom_call_target="tpu_custom_call" | custom-call | flops 10000000000 | bytes 16777216 | tf_op jit(solution)/shard_map/pallas_call | solution.py:211
  9.9 163.9 %while.27 = (s32[]{:T(128)}, f32[32,512]{1,0:T(8,128)S(1)}, f32[32,128]{1,0:T(8,128)S(1)}, f32[32,128]{1,0:T(8,128)S(1)}, f32[8,32,512]{2,1,0:T(8,128)S(1)}, /*i...) while((s32[]{:T(128)}, f32[32,512]{1,0:T(8,128)S(1)}, ...), condition=%wide.region_1.2_spmd, body=%wide.region_0.1_spmd.sunk | while | flops 103000236032 | bytes 78255016 | solution.py:307
  12.6 3.3 %collective-permute-start.1 = (f32[136,128]{1,0:T(8,128)S(1)}, f32[136,128]{1,0:T(8,128)S(1)}, u32[]{:S(2)}, u32[]{:S(2)}) collective-permute-start(f32[136,128]{1,0:T(8,128)S(1)} %get-tuple-element.486), channel_id=1, source_target_pairs={{0,64},{16,208},{32,96},{48,240},{64,128},{80,16},{96,160},{112,48... | collective-permute-start | bytes 208904 | tf_op jit(solution)/shard_map/while/body/eval_jaxpr/ppermute | solution.py:33
  15.8 4.0 %collective-permute-start.2 = (f32[136,128]{1,0:T(8,128)S(1)}, f32[136,128]{1,0:T(8,128)S(1)}, u32[]{:S(2)}, u32[]{:S(2)}) collective-permute-start(f32[136,128]{1,0:T(8,128)S(1)} %get-tuple-element.486), channel_id=1, source_target_pairs={{0,96},{16,176},{32,128},{48,208},{64,160},{80,240},{96,192},{112,... | collective-permute-start | bytes 208904 | tf_op jit(solution)/shard_map/while/body/eval_jaxpr/ppermute | solution.py:33
  24.2 3.6 %collective-permute-done.3 = f32[72,128]{1,0:T(8,128)S(1)} collective-permute-done((f32[72,128]{1,0:T(8,128)S(1)}, f32[72,128]{1,0:T(8,128)S(1)}, u32[]{:S(2)}, u32[]{:S(2)}) %collective-permute-start.3) | collective-permute-done | bytes 36896 | tf_op jit(solution)/shard_map/while/body/eval_jaxpr/ppermute | solution.py:33
  29.3 3.5 %eval_jaxpr.29 = (f32[136,128]{1,0:T(8,128)S(1)}, f32[8,32,512]{2,1,0:T(8,128)S(1)}, f32[32,512]{1,0:T(8,128)S(1)}) custom-call(s32[4]{0:T(128)S(1)} %pad_add_fusion.3.place, bf16[512,4096]{1,0:T(8,128)(2,1)S(1)} %copy-done, bf16[512,4096]{1,0:T(8,128)(2,1)S(1)} %copy-done.2, f32[32,512]{1,0:T(8,128)S(1)} %get-tuple-element.517.chip, ...), custom_call_target="tpu_custom_call" | custom-call | flops 1000000000 | bytes 8388608 | tf_op jit(solution)/shard_map/while/body/eval_jaxpr/pallas_call | solution.py:188
  40.8 3.1 %collective-permute-start.10 = (f32[136,128]{1,0:T(8,128)S(1)}, f32[136,128]{1,0:T(8,128)S(1)}, u32[]{:S(2)}, u32[]{:S(2)}) collective-permute-start(f32[136,128]{1,0:T(8,128)S(1)} %add_add_fusion.4.a), channel_id=1, source_target_pairs={{0,12},{4,0},{8,4},{12,8},{1,13},{5,1},{9,5},{13,9},{2,14},{6,2},{... | collective-permute-start | bytes 208904 | tf_op jit(solution)/shard_map/while/body/eval_jaxpr/ppermute | solution.py:40
  45.8 3.9 %collective-permute-done.8.b = f32[136,128]{1,0:T(8,128)S(1)} collective-permute-done((f32[136,128]{1,0:T(8,128)S(1)}, f32[136,128]{1,0:T(8,128)S(1)}, u32[]{:S(2)}, u32[]{:S(2)}) %collective-permute-start.8) | collective-permute-done | bytes 69664 | tf_op jit(solution)/shard_map/while/body/eval_jaxpr/ppermute | solution.py:40
  54.9 4.3 %collective-permute-start.13 = (f32[32,512]{1,0:T(8,128)S(1)}, f32[32,512]{1,0:T(8,128)S(1)}, u32[]{:S(2)}, u32[]{:S(2)}) collective-permute-start(f32[32,512]{1,0:T(8,128)S(1)} %get-tuple-element.494), channel_id=1, source_target_pairs={{0,96},{16,176},{32,128},{48,208},{64,160},{80,240},{96,192},{112,... | collective-permute-start | bytes 196616 | tf_op jit(solution)/shard_map/while/body/eval_jaxpr/ppermute | solution.py:33
  70.5 3.6 %collective-permute-start.2 = (f32[136,128]{1,0:T(8,128)S(1)}, f32[136,128]{1,0:T(8,128)S(1)}, u32[]{:S(2)}, u32[]{:S(2)}) collective-permute-start(f32[136,128]{1,0:T(8,128)S(1)} %get-tuple-element.486), channel_id=1, source_target_pairs={{0,96},{16,176},{32,128},{48,208},{64,160},{80,240},{96,192},{112,... | collective-permute-start | bytes 208904 | tf_op jit(solution)/shard_map/while/body/eval_jaxpr/ppermute | solution.py:33
  78.8 4.4 %collective-permute-done.3 = f32[72,128]{1,0:T(8,128)S(1)} collective-permute-done((f32[72,128]{1,0:T(8,128)S(1)}, f32[72,128]{1,0:T(8,128)S(1)}, u32[]{:S(2)}, u32[]{:S(2)}) %collective-permute-start.3) | collective-permute-done | bytes 36896 | tf_op jit(solution)/shard_map/while/body/eval_jaxpr/ppermute | solution.py:33
  84.7 3.5 %eval_jaxpr.29 = (f32[136,128]{1,0:T(8,128)S(1)}, f32[8,32,512]{2,1,0:T(8,128)S(1)}, f32[32,512]{1,0:T(8,128)S(1)}) custom-call(s32[4]{0:T(128)S(1)} %pad_add_fusion.3.place, bf16[512,4096]{1,0:T(8,128)(2,1)S(1)} %copy-done, bf16[512,4096]{1,0:T(8,128)(2,1)S(1)} %copy-done.2, f32[32,512]{1,0:T(8,128)S(1)} %get-tuple-element.517.chip, ...), custom_call_target="tpu_custom_call" | custom-call | flops 1000000000 | bytes 8388608 | tf_op jit(solution)/shard_map/while/body/eval_jaxpr/pallas_call | solution.py:188
  106.7 2.6 %collective-permute-start.12 = (f32[32,256]{1,0:T(8,128)S(1)}, f32[32,256]{1,0:T(8,128)S(1)}, u32[]{:S(2)}, u32[]{:S(2)}) collective-permute-start(f32[32,256]{1,0:T(8,128)S(1)} %slice.204), channel_id=1, source_target_pairs={{0,128},{16,144},{32,160},{48,176},{64,192},{80,208},{96,224},{112... | collective-permute-start | bytes 98312 | tf_op jit(solution)/shard_map/while/body/eval_jaxpr/ppermute | solution.py:33
  110.9 2.5 %collective-permute-start.14 = (f32[32,512]{1,0:T(8,128)S(1)}, f32[32,512]{1,0:T(8,128)S(1)}, u32[]{:S(2)}, u32[]{:S(2)}) collective-permute-start(f32[32,512]{1,0:T(8,128)S(1)} %get-tuple-element.495), channel_id=1, source_target_pairs={{0,32},{16,240},{32,64},{48,16},{64,96},{80,48},{96,128},{112,80},... | collective-permute-start | bytes 196616 | tf_op jit(solution)/shard_map/while/body/eval_jaxpr/ppermute | solution.py:33
  114.6 2.8 %collective-permute-done.13 = f32[32,512]{1,0:T(8,128)S(1)} collective-permute-done((f32[32,512]{1,0:T(8,128)S(1)}, f32[32,512]{1,0:T(8,128)S(1)}, u32[]{:S(2)}, u32[]{:S(2)}) %collective-permute-start.13) | collective-permute-done | bytes 65568 | tf_op jit(solution)/shard_map/while/body/eval_jaxpr/ppermute | solution.py:33
  125.5 2.9 %collective-permute-start.3 = (f32[72,128]{1,0:T(8,128)S(1)}, f32[72,128]{1,0:T(8,128)S(1)}, u32[]{:S(2)}, u32[]{:S(2)}) collective-permute-start(f32[72,128]{1,0:T(8,128)S(1)} %get-tuple-element.487), channel_id=1, source_target_pairs={{0,128},{16,144},{32,160},{48,176},{64,192},{80,208},{96,224},{112... | collective-permute-start | bytes 110600 | tf_op jit(solution)/shard_map/while/body/eval_jaxpr/ppermute | solution.py:33
  128.5 3.1 %collective-permute-done.2 = f32[136,128]{1,0:T(8,128)S(1)} collective-permute-done((f32[136,128]{1,0:T(8,128)S(1)}, f32[136,128]{1,0:T(8,128)S(1)}, u32[]{:S(2)}, u32[]{:S(2)}) %collective-permute-start.2) | collective-permute-done | bytes 69664 | tf_op jit(solution)/shard_map/while/body/eval_jaxpr/ppermute | solution.py:33
  135.0 3.5 %eval_jaxpr.29 = (f32[136,128]{1,0:T(8,128)S(1)}, f32[8,32,512]{2,1,0:T(8,128)S(1)}, f32[32,512]{1,0:T(8,128)S(1)}) custom-call(s32[4]{0:T(128)S(1)} %pad_add_fusion.3.place, bf16[512,4096]{1,0:T(8,128)(2,1)S(1)} %copy-done, bf16[512,4096]{1,0:T(8,128)(2,1)S(1)} %copy-done.2, f32[32,512]{1,0:T(8,128)S(1)} %get-tuple-element.517.chip, ...), custom_call_target="tpu_custom_call" | custom-call | flops 1000000000 | bytes 8388608 | tf_op jit(solution)/shard_map/while/body/eval_jaxpr/pallas_call | solution.py:188
  144.0 3.1 %collective-permute-done.7 = f32[136,128]{1,0:T(8,128)S(1)} collective-permute-done((f32[136,128]{1,0:T(8,128)S(1)}, f32[136,128]{1,0:T(8,128)S(1)}, u32[]{:S(2)}, u32[]{:S(2)}) %collective-permute-start.7) | collective-permute-done | bytes 69664 | tf_op jit(solution)/shard_map/while/body/eval_jaxpr/ppermute | solution.py:40
  151.6 3.2 %collective-permute-done.8.b = f32[136,128]{1,0:T(8,128)S(1)} collective-permute-done((f32[136,128]{1,0:T(8,128)S(1)}, f32[136,128]{1,0:T(8,128)S(1)}, u32[]{:S(2)}, u32[]{:S(2)}) %collective-permute-start.8) | collective-permute-done | bytes 69664 | tf_op jit(solution)/shard_map/while/body/eval_jaxpr/ppermute | solution.py:40
  158.7 3.2 %collective-permute-start.12 = (f32[32,256]{1,0:T(8,128)S(1)}, f32[32,256]{1,0:T(8,128)S(1)}, u32[]{:S(2)}, u32[]{:S(2)}) collective-permute-start(f32[32,256]{1,0:T(8,128)S(1)} %slice.204), channel_id=1, source_target_pairs={{0,128},{16,144},{32,160},{48,176},{64,192},{80,208},{96,224},{112... | collective-permute-start | bytes 98312 | tf_op jit(solution)/shard_map/while/body/eval_jaxpr/ppermute | solution.py:33
  161.9 3.0 %collective-permute-start.13 = (f32[32,512]{1,0:T(8,128)S(1)}, f32[32,512]{1,0:T(8,128)S(1)}, u32[]{:S(2)}, u32[]{:S(2)}) collective-permute-start(f32[32,512]{1,0:T(8,128)S(1)} %get-tuple-element.494), channel_id=1, source_target_pairs={{0,96},{16,176},{32,128},{48,208},{64,160},{80,240},{96,192},{112,... | collective-permute-start | bytes 196616 | tf_op jit(solution)/shard_map/while/body/eval_jaxpr/ppermute | solution.py:33
  165.4 3.4 %collective-permute-start.15 = (f32[32,512]{1,0:T(8,128)S(1)}, f32[32,512]{1,0:T(8,128)S(1)}, u32[]{:S(2)}, u32[]{:S(2)}) collective-permute-start(f32[32,512]{1,0:T(8,128)S(1)} %get-tuple-element.496), channel_id=1, source_target_pairs={{0,64},{16,208},{32,96},{48,240},{64,128},{80,16},{96,160},{112,48... | collective-permute-start | bytes 196616 | tf_op jit(solution)/shard_map/while/body/eval_jaxpr/ppermute | solution.py:33
  177.5 2.5 %collective-permute-start.21 = (f32[136,128]{1,0:T(8,128)S(1)}, f32[136,128]{1,0:T(8,128)S(1)}, u32[]{:S(2)}, u32[]{:S(2)}) collective-permute-start(f32[136,128]{1,0:T(8,128)S(1)} %get-tuple-element.331), channel_id=1, source_target_pairs={{0,96},{16,176},{32,128},{48,208},{64,160},{80,240},{96,192},{112,... | collective-permute-start | bytes 208904 | tf_op jit(solution)/shard_map/ppermute | solution.py:33
  180.0 2.9 %collective-permute-start.22 = (f32[72,128]{1,0:T(8,128)S(1)}, f32[72,128]{1,0:T(8,128)S(1)}, u32[]{:S(2)}, u32[]{:S(2)}) collective-permute-start(f32[72,128]{1,0:T(8,128)S(1)} %get-tuple-element.332), channel_id=1, source_target_pairs={{0,128},{16,144},{32,160},{48,176},{64,192},{80,208},{96,224},{112... | collective-permute-start | bytes 110600 | tf_op jit(solution)/shard_map/ppermute | solution.py:33
  182.9 2.7 %collective-permute-done.21 = f32[136,128]{1,0:T(8,128)S(1)} collective-permute-done((f32[136,128]{1,0:T(8,128)S(1)}, f32[136,128]{1,0:T(8,128)S(1)}, u32[]{:S(2)}, u32[]{:S(2)}) %collective-permute-start.21) | collective-permute-done | bytes 69664 | tf_op jit(solution)/shard_map/ppermute | solution.py:33
  185.6 3.2 %collective-permute-done.22 = f32[72,128]{1,0:T(8,128)S(1)} collective-permute-done((f32[72,128]{1,0:T(8,128)S(1)}, f32[72,128]{1,0:T(8,128)S(1)}, u32[]{:S(2)}, u32[]{:S(2)}) %collective-permute-start.22) | collective-permute-done | bytes 36896 | tf_op jit(solution)/shard_map/ppermute | solution.py:33
  190.4 3.5 %shard_map.87 = (f32[136,128]{1,0:T(8,128)S(1)}, f32[8,32,512]{2,1,0:T(8,128)S(1)}, f32[32,512]{1,0:T(8,128)S(1)}) custom-call(s32[4]{0:T(128)S(1)} %pad_add_fusion.1.place, bf16[512,4096]{1,0:T(8,128)(2,1)S(1)} %copy-done.1, bf16[512,4096]{1,0:T(8,128)(2,1)S(1)} %copy-done.3, f32[32,512]{1,0:T(8,128)S(1)} %get-tuple-element.329.chip, ...), custom_call_target="tpu_custom_call" | custom-call | flops 1000000000 | bytes 8388608 | tf_op jit(solution)/shard_map/pallas_call | solution.py:188
  193.9 2.9 %collective-permute-start.24 = (f32[136,128]{1,0:T(8,128)S(1)}, f32[136,128]{1,0:T(8,128)S(1)}, u32[]{:S(2)}, u32[]{:S(2)}) collective-permute-start(f32[136,128]{1,0:T(8,128)S(1)} %get-tuple-element.338), channel_id=1, source_target_pairs={{0,2},{1,3},{2,0},{3,1},{4,6},{5,7},{6,4},{7,5},{8,10},{9,11},{10,... | collective-permute-start | bytes 208904 | tf_op jit(solution)/shard_map/ppermute | solution.py:40
  204.3 3.2 %collective-permute-start.29 = (f32[136,128]{1,0:T(8,128)S(1)}, f32[136,128]{1,0:T(8,128)S(1)}, u32[]{:S(2)}, u32[]{:S(2)}) collective-permute-start(f32[136,128]{1,0:T(8,128)S(1)} %add_add_fusion.2), channel_id=1, source_target_pairs={{0,12},{4,0},{8,4},{12,8},{1,13},{5,1},{9,5},{13,9},{2,14},{6,2},{... | collective-permute-start | bytes 208904 | tf_op jit(solution)/shard_map/ppermute | solution.py:40
  210.6 4.8 %all-to-all-start = ((f32[16,8,128]{2,1,0:T(8,128)}), f32[16,8,128]{2,1,0:T(8,128)S(1)}, u32[]{:S(2)}, u32[]{:S(2)}) async-start(f32[16,8,128]{2,1,0:T(8,128)} %broadcast_in_dim.22), calls=%async_computation | async-start | bytes 131072 | tf_op jit(solution)/shard_map/all_to_all | solution.py:318
  215.4 7.8 %all-to-all-done = f32[16,8,128]{2,1,0:T(8,128)S(1)} async-done(((f32[16,8,128]{2,1,0:T(8,128)}), f32[16,8,128]{2,1,0:T(8,128)S(1)}, u32[]{:S(2)}, u32[]{:S(2)}) %all-to-all-start) | async-done | bytes 65568 | tf_op jit(solution)/shard_map/all_to_all | solution.py:318
  (221 shorter events, 111.9 us)
Async XLA Ops:
  0.6 9.1 %collective-permute-start.17 = (f32[32,256]{1,0:T(8,128)}, f32[32,256]{1,0:T(8,128)S(1)}, u32[]{:S(2)}, u32[]{:S(2)}) collective-permute-start(f32[32,256]{1,0:T(8,128)} %param.10), channel_id=1, source_target_pairs={{0,16},{16,0},{1,17},{17,1},{2,18},{18,2},{3,19},{19,3},{4,20},{20... | collective-permute-start | bytes 98312 | tf_op jit(solution)/shard_map/ppermute | solution.py:25
  1.5 8.2 %collective-permute-start.18 = (f32[32,256]{1,0:T(8,128)S(1)}, f32[32,256]{1,0:T(8,128)S(1)}, u32[]{:S(2)}, u32[]{:S(2)}) collective-permute-start(f32[32,256]{1,0:T(8,128)S(1)} %subtract_multiply_fusion), channel_id=1, source_target_pairs={{0,16},{16,0},{1,17},{17,1},{2,18},{18,2},{3,19},{19,3},{4,20},{20... | collective-permute-start | bytes 98312 | tf_op jit(solution)/shard_map/ppermute | solution.py:25
  10.6 9.8 %collective-permute-start = (f32[136,128]{1,0:T(8,128)S(1)}, f32[136,128]{1,0:T(8,128)S(1)}, u32[]{:S(2)}, u32[]{:S(2)}) collective-permute-start(f32[136,128]{1,0:T(8,128)S(1)} %get-tuple-element.486), channel_id=1, source_target_pairs={{0,32},{16,240},{32,64},{48,16},{64,96},{80,48},{96,128},{112,80},... | collective-permute-start | bytes 208904 | tf_op jit(solution)/shard_map/while/body/eval_jaxpr/ppermute | solution.py:33
  12.6 9.2 %collective-permute-start.1 = (f32[136,128]{1,0:T(8,128)S(1)}, f32[136,128]{1,0:T(8,128)S(1)}, u32[]{:S(2)}, u32[]{:S(2)}) collective-permute-start(f32[136,128]{1,0:T(8,128)S(1)} %get-tuple-element.486), channel_id=1, source_target_pairs={{0,64},{16,208},{32,96},{48,240},{64,128},{80,16},{96,160},{112,48... | collective-permute-start | bytes 208904 | tf_op jit(solution)/shard_map/while/body/eval_jaxpr/ppermute | solution.py:33
  15.8 8.3 %collective-permute-start.2 = (f32[136,128]{1,0:T(8,128)S(1)}, f32[136,128]{1,0:T(8,128)S(1)}, u32[]{:S(2)}, u32[]{:S(2)}) collective-permute-start(f32[136,128]{1,0:T(8,128)S(1)} %get-tuple-element.486), channel_id=1, source_target_pairs={{0,96},{16,176},{32,128},{48,208},{64,160},{80,240},{96,192},{112,... | collective-permute-start | bytes 208904 | tf_op jit(solution)/shard_map/while/body/eval_jaxpr/ppermute | solution.py:33
  19.9 7.9 %collective-permute-start.3 = (f32[72,128]{1,0:T(8,128)S(1)}, f32[72,128]{1,0:T(8,128)S(1)}, u32[]{:S(2)}, u32[]{:S(2)}) collective-permute-start(f32[72,128]{1,0:T(8,128)S(1)} %get-tuple-element.487), channel_id=1, source_target_pairs={{0,128},{16,144},{32,160},{48,176},{64,192},{80,208},{96,224},{112... | collective-permute-start | bytes 110600 | tf_op jit(solution)/shard_map/while/body/eval_jaxpr/ppermute | solution.py:33
  53.5 8.2 %collective-permute-start.12 = (f32[32,256]{1,0:T(8,128)S(1)}, f32[32,256]{1,0:T(8,128)S(1)}, u32[]{:S(2)}, u32[]{:S(2)}) collective-permute-start(f32[32,256]{1,0:T(8,128)S(1)} %slice.204), channel_id=1, source_target_pairs={{0,128},{16,144},{32,160},{48,176},{64,192},{80,208},{96,224},{112... | collective-permute-start | bytes 98312 | tf_op jit(solution)/shard_map/while/body/eval_jaxpr/ppermute | solution.py:33
  54.9 8.8 %collective-permute-start.13 = (f32[32,512]{1,0:T(8,128)S(1)}, f32[32,512]{1,0:T(8,128)S(1)}, u32[]{:S(2)}, u32[]{:S(2)}) collective-permute-start(f32[32,512]{1,0:T(8,128)S(1)} %get-tuple-element.494), channel_id=1, source_target_pairs={{0,96},{16,176},{32,128},{48,208},{64,160},{80,240},{96,192},{112,... | collective-permute-start | bytes 196616 | tf_op jit(solution)/shard_map/while/body/eval_jaxpr/ppermute | solution.py:33
  60.2 6.8 %collective-permute-start.15 = (f32[32,512]{1,0:T(8,128)S(1)}, f32[32,512]{1,0:T(8,128)S(1)}, u32[]{:S(2)}, u32[]{:S(2)}) collective-permute-start(f32[32,512]{1,0:T(8,128)S(1)} %get-tuple-element.496), channel_id=1, source_target_pairs={{0,64},{16,208},{32,96},{48,240},{64,128},{80,16},{96,160},{112,48... | collective-permute-start | bytes 196616 | tf_op jit(solution)/shard_map/while/body/eval_jaxpr/ppermute | solution.py:33
  69.1 7.3 %collective-permute-start = (f32[136,128]{1,0:T(8,128)S(1)}, f32[136,128]{1,0:T(8,128)S(1)}, u32[]{:S(2)}, u32[]{:S(2)}) collective-permute-start(f32[136,128]{1,0:T(8,128)S(1)} %get-tuple-element.486), channel_id=1, source_target_pairs={{0,32},{16,240},{32,64},{48,16},{64,96},{80,48},{96,128},{112,80},... | collective-permute-start | bytes 208904 | tf_op jit(solution)/shard_map/while/body/eval_jaxpr/ppermute | solution.py:33
  70.4 8.4 %collective-permute-start.1 = (f32[136,128]{1,0:T(8,128)S(1)}, f32[136,128]{1,0:T(8,128)S(1)}, u32[]{:S(2)}, u32[]{:S(2)}) collective-permute-start(f32[136,128]{1,0:T(8,128)S(1)} %get-tuple-element.486), channel_id=1, source_target_pairs={{0,64},{16,208},{32,96},{48,240},{64,128},{80,16},{96,160},{112,48... | collective-permute-start | bytes 208904 | tf_op jit(solution)/shard_map/while/body/eval_jaxpr/ppermute | solution.py:33
  70.5 8.3 %collective-permute-start.2 = (f32[136,128]{1,0:T(8,128)S(1)}, f32[136,128]{1,0:T(8,128)S(1)}, u32[]{:S(2)}, u32[]{:S(2)}) collective-permute-start(f32[136,128]{1,0:T(8,128)S(1)} %get-tuple-element.486), channel_id=1, source_target_pairs={{0,96},{16,176},{32,128},{48,208},{64,160},{80,240},{96,192},{112,... | collective-permute-start | bytes 208904 | tf_op jit(solution)/shard_map/while/body/eval_jaxpr/ppermute | solution.py:33
  74.0 9.1 %collective-permute-start.3 = (f32[72,128]{1,0:T(8,128)S(1)}, f32[72,128]{1,0:T(8,128)S(1)}, u32[]{:S(2)}, u32[]{:S(2)}) collective-permute-start(f32[72,128]{1,0:T(8,128)S(1)} %get-tuple-element.487), channel_id=1, source_target_pairs={{0,128},{16,144},{32,160},{48,176},{64,192},{80,208},{96,224},{112... | collective-permute-start | bytes 110600 | tf_op jit(solution)/shard_map/while/body/eval_jaxpr/ppermute | solution.py:33
  96.7 6.3 %collective-permute-start.8 = (f32[136,128]{1,0:T(8,128)S(1)}, f32[136,128]{1,0:T(8,128)S(1)}, u32[]{:S(2)}, u32[]{:S(2)}) collective-permute-start(f32[136,128]{1,0:T(8,128)S(1)} %add_add_fusion.4.a), channel_id=1, source_target_pairs={{0,8},{4,12},{8,0},{12,4},{1,9},{5,13},{9,1},{13,5},{2,10},{6,14},... | collective-permute-start | bytes 208904 | tf_op jit(solution)/shard_map/while/body/eval_jaxpr/ppermute | solution.py:40
  97.6 6.0 %collective-permute-start.9 = (f32[136,128]{1,0:T(8,128)S(1)}, f32[136,128]{1,0:T(8,128)S(1)}, u32[]{:S(2)}, u32[]{:S(2)}) collective-permute-start(f32[136,128]{1,0:T(8,128)S(1)} %add_add_fusion.4.a), channel_id=1, source_target_pairs={{0,4},{4,8},{8,12},{12,0},{1,5},{5,9},{9,13},{13,1},{2,6},{6,10},{... | collective-permute-start | bytes 208904 | tf_op jit(solution)/shard_map/while/body/eval_jaxpr/ppermute | solution.py:40
  106.7 7.9 %collective-permute-start.12 = (f32[32,256]{1,0:T(8,128)S(1)}, f32[32,256]{1,0:T(8,128)S(1)}, u32[]{:S(2)}, u32[]{:S(2)}) collective-permute-start(f32[32,256]{1,0:T(8,128)S(1)} %slice.204), channel_id=1, source_target_pairs={{0,128},{16,144},{32,160},{48,176},{64,192},{80,208},{96,224},{112... | collective-permute-start | bytes 98312 | tf_op jit(solution)/shard_map/while/body/eval_jaxpr/ppermute | solution.py:33
  109.4 8.1 %collective-permute-start.13 = (f32[32,512]{1,0:T(8,128)S(1)}, f32[32,512]{1,0:T(8,128)S(1)}, u32[]{:S(2)}, u32[]{:S(2)}) collective-permute-start(f32[32,512]{1,0:T(8,128)S(1)} %get-tuple-element.494), channel_id=1, source_target_pairs={{0,96},{16,176},{32,128},{48,208},{64,160},{80,240},{96,192},{112,... | collective-permute-start | bytes 196616 | tf_op jit(solution)/shard_map/while/body/eval_jaxpr/ppermute | solution.py:33
  110.9 6.6 %collective-permute-start.14 = (f32[32,512]{1,0:T(8,128)S(1)}, f32[32,512]{1,0:T(8,128)S(1)}, u32[]{:S(2)}, u32[]{:S(2)}) collective-permute-start(f32[32,512]{1,0:T(8,128)S(1)} %get-tuple-element.495), channel_id=1, source_target_pairs={{0,32},{16,240},{32,64},{48,16},{64,96},{80,48},{96,128},{112,80},... | collective-permute-start | bytes 196616 | tf_op jit(solution)/shard_map/while/body/eval_jaxpr/ppermute | solution.py:33
  113.4 6.4 %collective-permute-start.15 = (f32[32,512]{1,0:T(8,128)S(1)}, f32[32,512]{1,0:T(8,128)S(1)}, u32[]{:S(2)}, u32[]{:S(2)}) collective-permute-start(f32[32,512]{1,0:T(8,128)S(1)} %get-tuple-element.496), channel_id=1, source_target_pairs={{0,64},{16,208},{32,96},{48,240},{64,128},{80,16},{96,160},{112,48... | collective-permute-start | bytes 196616 | tf_op jit(solution)/shard_map/while/body/eval_jaxpr/ppermute | solution.py:33
  121.9 6.5 %collective-permute-start = (f32[136,128]{1,0:T(8,128)S(1)}, f32[136,128]{1,0:T(8,128)S(1)}, u32[]{:S(2)}, u32[]{:S(2)}) collective-permute-start(f32[136,128]{1,0:T(8,128)S(1)} %get-tuple-element.486), channel_id=1, source_target_pairs={{0,32},{16,240},{32,64},{48,16},{64,96},{80,48},{96,128},{112,80},... | collective-permute-start | bytes 208904 | tf_op jit(solution)/shard_map/while/body/eval_jaxpr/ppermute | solution.py:33
  121.9 6.6 %collective-permute-start.1 = (f32[136,128]{1,0:T(8,128)S(1)}, f32[136,128]{1,0:T(8,128)S(1)}, u32[]{:S(2)}, u32[]{:S(2)}) collective-permute-start(f32[136,128]{1,0:T(8,128)S(1)} %get-tuple-element.486), channel_id=1, source_target_pairs={{0,64},{16,208},{32,96},{48,240},{64,128},{80,16},{96,160},{112,48... | collective-permute-start | bytes 208904 | tf_op jit(solution)/shard_map/while/body/eval_jaxpr/ppermute | solution.py:33
  123.5 8.1 %collective-permute-start.2 = (f32[136,128]{1,0:T(8,128)S(1)}, f32[136,128]{1,0:T(8,128)S(1)}, u32[]{:S(2)}, u32[]{:S(2)}) collective-permute-start(f32[136,128]{1,0:T(8,128)S(1)} %get-tuple-element.486), channel_id=1, source_target_pairs={{0,96},{16,176},{32,128},{48,208},{64,160},{80,240},{96,192},{112,... | collective-permute-start | bytes 208904 | tf_op jit(solution)/shard_map/while/body/eval_jaxpr/ppermute | solution.py:33
  125.5 8.0 %collective-permute-start.3 = (f32[72,128]{1,0:T(8,128)S(1)}, f32[72,128]{1,0:T(8,128)S(1)}, u32[]{:S(2)}, u32[]{:S(2)}) collective-permute-start(f32[72,128]{1,0:T(8,128)S(1)} %get-tuple-element.487), channel_id=1, source_target_pairs={{0,128},{16,144},{32,160},{48,176},{64,192},{80,208},{96,224},{112... | collective-permute-start | bytes 110600 | tf_op jit(solution)/shard_map/while/body/eval_jaxpr/ppermute | solution.py:33
  158.7 10.0 %collective-permute-start.12 = (f32[32,256]{1,0:T(8,128)S(1)}, f32[32,256]{1,0:T(8,128)S(1)}, u32[]{:S(2)}, u32[]{:S(2)}) collective-permute-start(f32[32,256]{1,0:T(8,128)S(1)} %slice.204), channel_id=1, source_target_pairs={{0,128},{16,144},{32,160},{48,176},{64,192},{80,208},{96,224},{112... | collective-permute-start | bytes 98312 | tf_op jit(solution)/shard_map/while/body/eval_jaxpr/ppermute | solution.py:33
  161.9 8.8 %collective-permute-start.13 = (f32[32,512]{1,0:T(8,128)S(1)}, f32[32,512]{1,0:T(8,128)S(1)}, u32[]{:S(2)}, u32[]{:S(2)}) collective-permute-start(f32[32,512]{1,0:T(8,128)S(1)} %get-tuple-element.494), channel_id=1, source_target_pairs={{0,96},{16,176},{32,128},{48,208},{64,160},{80,240},{96,192},{112,... | collective-permute-start | bytes 196616 | tf_op jit(solution)/shard_map/while/body/eval_jaxpr/ppermute | solution.py:33
  164.9 6.3 %collective-permute-start.14 = (f32[32,512]{1,0:T(8,128)S(1)}, f32[32,512]{1,0:T(8,128)S(1)}, u32[]{:S(2)}, u32[]{:S(2)}) collective-permute-start(f32[32,512]{1,0:T(8,128)S(1)} %get-tuple-element.495), channel_id=1, source_target_pairs={{0,32},{16,240},{32,64},{48,16},{64,96},{80,48},{96,128},{112,80},... | collective-permute-start | bytes 196616 | tf_op jit(solution)/shard_map/while/body/eval_jaxpr/ppermute | solution.py:33
  165.4 6.8 %collective-permute-start.15 = (f32[32,512]{1,0:T(8,128)S(1)}, f32[32,512]{1,0:T(8,128)S(1)}, u32[]{:S(2)}, u32[]{:S(2)}) collective-permute-start(f32[32,512]{1,0:T(8,128)S(1)} %get-tuple-element.496), channel_id=1, source_target_pairs={{0,64},{16,208},{32,96},{48,240},{64,128},{80,16},{96,160},{112,48... | collective-permute-start | bytes 196616 | tf_op jit(solution)/shard_map/while/body/eval_jaxpr/ppermute | solution.py:33
  174.4 8.5 %collective-permute-start.19 = (f32[136,128]{1,0:T(8,128)S(1)}, f32[136,128]{1,0:T(8,128)S(1)}, u32[]{:S(2)}, u32[]{:S(2)}) collective-permute-start(f32[136,128]{1,0:T(8,128)S(1)} %get-tuple-element.331), channel_id=1, source_target_pairs={{0,32},{16,240},{32,64},{48,16},{64,96},{80,48},{96,128},{112,80},... | collective-permute-start | bytes 208904 | tf_op jit(solution)/shard_map/ppermute | solution.py:33
  176.3 6.6 %collective-permute-start.20 = (f32[136,128]{1,0:T(8,128)S(1)}, f32[136,128]{1,0:T(8,128)S(1)}, u32[]{:S(2)}, u32[]{:S(2)}) collective-permute-start(f32[136,128]{1,0:T(8,128)S(1)} %get-tuple-element.331), channel_id=1, source_target_pairs={{0,64},{16,208},{32,96},{48,240},{64,128},{80,16},{96,160},{112,48... | collective-permute-start | bytes 208904 | tf_op jit(solution)/shard_map/ppermute | solution.py:33
  177.5 8.2 %collective-permute-start.21 = (f32[136,128]{1,0:T(8,128)S(1)}, f32[136,128]{1,0:T(8,128)S(1)}, u32[]{:S(2)}, u32[]{:S(2)}) collective-permute-start(f32[136,128]{1,0:T(8,128)S(1)} %get-tuple-element.331), channel_id=1, source_target_pairs={{0,96},{16,176},{32,128},{48,208},{64,160},{80,240},{96,192},{112,... | collective-permute-start | bytes 208904 | tf_op jit(solution)/shard_map/ppermute | solution.py:33
  180.0 8.8 %collective-permute-start.22 = (f32[72,128]{1,0:T(8,128)S(1)}, f32[72,128]{1,0:T(8,128)S(1)}, u32[]{:S(2)}, u32[]{:S(2)}) collective-permute-start(f32[72,128]{1,0:T(8,128)S(1)} %get-tuple-element.332), channel_id=1, source_target_pairs={{0,128},{16,144},{32,160},{48,176},{64,192},{80,208},{96,224},{112... | collective-permute-start | bytes 110600 | tf_op jit(solution)/shard_map/ppermute | solution.py:33
  210.6 12.6 %all-to-all-start = ((f32[16,8,128]{2,1,0:T(8,128)}), f32[16,8,128]{2,1,0:T(8,128)S(1)}, u32[]{:S(2)}, u32[]{:S(2)}) async-start(f32[16,8,128]{2,1,0:T(8,128)} %broadcast_in_dim.22), calls=%async_computation | async-start | bytes 131072 | tf_op jit(solution)/shard_map/all_to_all | solution.py:318
  (45 other events, 322.0 us)
where the time goes:
time: 227 us; the launch traced here: 225 us
  starting transfers between devices  96.5 us (43%)
  waiting for transfers between devices  89.7 us (40%)
  Pallas kernels  32.6 us (14%)
  other arithmetic  3.08 us (1%)
    ppermute x28, starting transfers between devices, along_z(): return lax.ppermute(x, ROW, table)  57.9 us
    ppermute x28, waiting for transfers between devices, along_z(): return lax.ppermute(x, ROW, table)  39.2 us
    ppermute x24, waiting for transfers between devices, ring_parts(): parts.append(lax.ppermute(x, axis, [(i, (i + k) % n) for i in range(n)]))  32.9 us
    ppermute x24, starting transfers between devices, ring_parts(): parts.append(lax.ppermute(x, axis, [(i, (i + k) % n) for i in range(n)]))  32.8 us
    pallas_call x14, Pallas kernels, call(): pl.pallas_call(kernel, in_specs=kinds + [VMEM] * (len(args) - len(kinds))...  25.1 us
    ppermute x12, waiting for transfers between devices, pair(): return lax.ppermute(x, 'row_1', [(0, 1), (1, 0)])  9.86 us
    all_to_all x1, waiting for transfers between devices, on_device(): lax.all_to_all(jnp.broadcast_to(part, (16, 8, S)), ROW, 0, 0, tiled=True)  7.78 us
    pallas_call x1, Pallas kernels, prepare(): pl.pallas_call(prepare_kernel, grid=(Z // 2,), in_specs=[block], out_spec...  7.51 us
  transfers between devices with their start and end apart: 65, of which 53 were waited for; matrix products, arithmetic and copies ran while one was open for 1% of the time, Pallas kernels for 5%

commit v1 on v0

--- a/solution.py
+++ b/solution.py
@@ -28,7 +28,8 @@
 def along_z(x, k):
     table = []
     for z in range(Z):
-        table.append((2 * z, 2 * ((z + k) % Z)))
+        if k < Z // 2:
+            table.append((2 * z, 2 * ((z + k) % Z)))
         table.append((2 * z + 1, 2 * ((z - k) % Z) + 1))
     return lax.ppermute(x, ROW, table)
 
@@ -90,8 +91,8 @@
     out, after, found_out, both, acc, top,
 ):
     early = place[3] < 2
-    total = mine[3 * T + 2 * K :]
-    for i in range(3):
+    total = jnp.zeros((8, S), jnp.float32)
+    for i in range(4):
         at = slice(i * T + 4 * K, (i + 1) * T)
         total = total + (mine[at] + theirs[at])
     total = part[...] + restored(total)
@@ -99,7 +100,6 @@
     alpha = jnp.where(early, -1.0, alpha)
     kept = jnp.where(early, 0.0, 1.0)
     found_out[...] = found[...] + alpha * direction[0]
-    first = place[2] == 0
     R = 16
     tops = []
 
@@ -118,8 +118,7 @@
             elif j > 4:
                 value = piece(theirs, 7 - j, 4, i)
             else:
-                a, b = piece(mine, 3, 2, i), piece(theirs, 3, 2, i)
-                value = jnp.concatenate([jnp.where(first, a, b), jnp.where(first, b, a)], 1)
+                value = piece(mine, 3, 4, i) + piece(theirs, 3, 4, i)
             old = direction[j, rows, :]
             value = kept * before[j, rows, :] - alpha[i * R : i * R + R] * (value + penalty * old)
             after[j, rows, :] = value
@@ -144,11 +143,8 @@
     for i in range(3):
         at = columns(place, side * (i + 1))
         out[:, i * W : (i + 1) * W] = product(both, hi[:, at], lo[:, at], False)
-    for i in range(2):
-        start = lax.rem(place[0] + Z // 2 * (1 - i), Z) * W + which * H
-        at = pl.ds(pl.multiple_of(start, H), H)
-        spot = 3 * W + i * H
-        out[:, spot : spot + H] = product(both, hi[:, at], lo[:, at], False)
+    at = columns(place, Z // 2 * which)
+    out[:, 3 * W : 4 * W] = product(both, hi[:, at], lo[:, at], False)
     out[:, 4 * W :] = lanes(row_sums(values * values))
 
 
@@ -219,15 +215,10 @@
     )(design)
 
 
-def pack_kernel(place, chip, extra, whole, small):
-    tile = flipped(extra[...])
+def pack_kernel(chip, extra, whole):
     for c in range(4):
         whole[c * K : (c + 1) * K] = chip[:, c * S : (c + 1) * S]
-    whole[4 * K :] = tile
-    for c in range(2):
-        one, two = chip[:, c * S : (c + 1) * S], chip[:, H + c * S : H + (c + 1) * S]
-        small[c * K : (c + 1) * K] = jnp.where(place[2] == 0, one, two)
-    small[2 * K :] = tile
+    whole[4 * K :] = flipped(extra[...])
 
 
 def forward(*args):
@@ -252,22 +243,20 @@
     def joined(mine, other):
         return jnp.where(core == 0, jnp.concatenate([mine, other], 1), jnp.concatenate([other, mine], 1))
 
-    def gathered(at, chip, extra):
-        outs = [array(T, S), array(2 * K + 8, S)]
-        whole, small = call(pack_kernel, [SMEM], outs, [], 24, at, chip, extra, flops=10**11)
+    def gathered(chip, extra):
+        (whole,) = call(pack_kernel, [], [array(T, S)], [], 24, chip, extra, flops=10**11)
         parts = {}
         for k in (4, 3, 2, 1):
-            parts[k] = along_z(small if k == 4 else whole, k)
+            parts[k] = along_z(whole, k)
         mine = jnp.concatenate([parts[k] for k in (1, 2, 3, 4)], 0)
         return mine, pair(mine)
 
     def reduced(both):
-        got4 = along_z(both[:, 3 * W : 3 * W + H], 4)
+        got4 = along_z(both[:, 3 * W : 4 * W], 4)
         got3 = along_z(both[:, 2 * W : 3 * W], 3)
         got2 = along_z(both[:, W : 2 * W], 2)
         got1 = along_z(both[:, :W], 1)
-        mine = got4 + both[:, 3 * W + H : 4 * W]
-        side = (got1 + got2 + got3) + joined(mine, jnp.zeros_like(mine))
+        side = (got1 + got2 + got3) + jnp.where(core == 0, both[:, 3 * W : 4 * W], got4)
         return side + pair(side), both[:, 4 * W :]
 
     def plane(x):
@@ -285,7 +274,7 @@
     def ahead(turn, carry):
         chip, part, state, residual, direction, found, _ = carry
         at = place(turn)
-        mine, theirs = gathered(at, chip, part)
+        mine, theirs = gathered(chip, part)
         value, residual, found = forward(
             at, hi, lo, chip, mine, theirs, state, part, residual, direction, found
         )

time: 227 us -> 227 us (level)
  starting transfers between devices: 96.5 us -> 103 us
  waiting for transfers between devices: 89.7 us -> 85.3 us
    ppermute x12, starting transfers between devices: 0.98 us -> 23.1 us  [pair(): return lax.ppermute(x, 'row_1', [(0, 1), (1, 0)])]
    ppermute x28, starting transfers between devices: 57.9 us -> 42.8 us  [along_z(): return lax.ppermute(x, ROW, table)]
    ppermute x12, waiting for transfers between devices: 9.86 us -> 7.29 us  [pair(): return lax.ppermute(x, 'row_1', [(0, 1), (1, 0)])]
  transfers between devices with their start and end apart: 65 -> 65, of which waited for: 53 -> 52; matrix products, arithmetic and copies ran while one was open for 1% -> 1% of each run, Pallas kernels for 5% -> 5%
where the time goes in v1:
time: 227 us; the launch traced here: 224 us
  starting transfers between devices  103 us (45%)
  waiting for transfers between devices  85.3 us (38%)
  Pallas kernels  30.4 us (13%)
  other arithmetic  3.06 us (1%)
    ppermute x28, starting transfers between devices, along_z(): return lax.ppermute(x, ROW, table)  42.8 us
    ppermute x28, waiting for transfers between devices, along_z(): return lax.ppermute(x, ROW, table)  37.5 us
    ppermute x24, starting transfers between devices, ring_parts(): parts.append(lax.ppermute(x, axis, [(i, (i + k) % n) for i in range(n)]))  33 us
    ppermute x24, waiting for transfers between devices, ring_parts(): parts.append(lax.ppermute(x, axis, [(i, (i + k) % n) for i in range(n)]))  32.7 us
    ppermute x12, starting transfers between devices, pair(): return lax.ppermute(x, 'row_1', [(0, 1), (1, 0)])  23.1 us
    pallas_call x14, Pallas kernels, call(): pl.pallas_call(kernel, in_specs=kinds + [VMEM] * (len(args) - len(kinds))...  22.9 us
    all_to_all x1, waiting for transfers between devices, on_device(): lax.all_to_all(jnp.broadcast_to(part, (16, 8, S)), ROW, 0, 0, tiled=True)  7.78 us
    pallas_call x1, Pallas kernels, prepare(): pl.pallas_call(prepare_kernel, grid=(Z // 2,), in_specs=[block], out_spec...  7.56 us
  transfers between devices with their start and end apart: 65, of which 52 were waited for; matrix products, arithmetic and copies ran while one was open for 1% of the time, Pallas kernels for 5%

profile of v1, /device:TPU:2, one launch (start us, length us, event | category | flops | bytes accessed | tf_op | source)
XLA Modules:
  0.0 224.4 jit_solution(2840774434934308440)
XLA Ops:
  2.1 7.6 %shard_map.85 = (bf16[512,4096]{1,0:T(8,128)(2,1)}, bf16[512,4096]{1,0:T(8,128)(2,1)}) custom-call(f32[512,4096]{1,0:T(8,128)} %design.1), custom_call_target="tpu_custom_call" | custom-call | flops 10000000000 | bytes 16777216 | tf_op jit(solution)/shard_map/pallas_call | solution.py:207
  9.9 164.6 %while.27 = (s32[]{:T(128)}, f32[32,512]{1,0:T(8,128)S(1)}, f32[32,128]{1,0:T(8,128)S(1)}, f32[32,128]{1,0:T(8,128)S(1)}, f32[8,32,512]{2,1,0:T(8,128)S(1)}, /*i...) while((s32[]{:T(128)}, f32[32,512]{1,0:T(8,128)S(1)}, ...), condition=%wide.region_1.2_spmd, body=%wide.region_0.1_spmd.sunk | while | flops 103000227840 | bytes 78779304 | solution.py:296
  12.0 3.3 %collective-permute-start.1 = (f32[136,128]{1,0:T(8,128)S(1)}, f32[136,128]{1,0:T(8,128)S(1)}, u32[]{:S(2)}, u32[]{:S(2)}) collective-permute-start(f32[136,128]{1,0:T(8,128)S(1)} %eval_jaxpr.28), channel_id=1, source_target_pairs={{0,64},{16,208},{32,96},{48,240},{64,128},{80,16},{96,160},{112,48... | collective-permute-start | bytes 208904 | tf_op jit(solution)/shard_map/while/body/eval_jaxpr/ppermute | solution.py:34
  15.2 4.0 %collective-permute-start.2 = (f32[136,128]{1,0:T(8,128)S(1)}, f32[136,128]{1,0:T(8,128)S(1)}, u32[]{:S(2)}, u32[]{:S(2)}) collective-permute-start(f32[136,128]{1,0:T(8,128)S(1)} %eval_jaxpr.28), channel_id=1, source_target_pairs={{0,96},{16,176},{32,128},{48,208},{64,160},{80,240},{96,192},{112,... | collective-permute-start | bytes 208904 | tf_op jit(solution)/shard_map/while/body/eval_jaxpr/ppermute | solution.py:34
  23.6 3.0 %collective-permute-start.4 = (f32[544,128]{1,0:T(8,128)S(1)}, f32[544,128]{1,0:T(8,128)S(1)}, u32[]{:S(2)}, u32[]{:S(2)}) collective-permute-start(f32[544,128]{1,0:T(8,128)S(1)} %constant_dynamic-update-slice_fusion.15.mine), channel_id=1, source_target_pairs={{0,16},{16,0},{1,17},{17,1},{2,18},{18,2},{3,19},{19,3},{4,20},{20... | collective-permute-start | bytes 835592 | tf_op jit(solution)/shard_map/while/body/eval_jaxpr/ppermute | solution.py:25
  27.8 3.5 %eval_jaxpr.29 = (f32[136,128]{1,0:T(8,128)S(1)}, f32[8,32,512]{2,1,0:T(8,128)S(1)}, f32[32,512]{1,0:T(8,128)S(1)}) custom-call(s32[4]{0:T(128)S(1)} %pad_add_fusion.3.place, bf16[512,4096]{1,0:T(8,128)(2,1)S(1)} %copy-done, bf16[512,4096]{1,0:T(8,128)(2,1)S(1)} %copy-done.2, f32[32,512]{1,0:T(8,128)S(1)} %get-tuple-element.510.chip, ...), custom_call_target="tpu_custom_call" | custom-call | flops 1000000000 | bytes 8388608 | tf_op jit(solution)/shard_map/while/body/eval_jaxpr/pallas_call | solution.py:184
  39.3 3.1 %collective-permute-start.10 = (f32[136,128]{1,0:T(8,128)S(1)}, f32[136,128]{1,0:T(8,128)S(1)}, u32[]{:S(2)}, u32[]{:S(2)}) collective-permute-start(f32[136,128]{1,0:T(8,128)S(1)} %add_add_fusion.4.a), channel_id=1, source_target_pairs={{0,12},{4,0},{8,4},{12,8},{1,13},{5,1},{9,5},{13,9},{2,14},{6,2},{... | collective-permute-start | bytes 208904 | tf_op jit(solution)/shard_map/while/body/eval_jaxpr/ppermute | solution.py:41
  44.3 3.9 %collective-permute-done.8.b = f32[136,128]{1,0:T(8,128)S(1)} collective-permute-done((f32[136,128]{1,0:T(8,128)S(1)}, f32[136,128]{1,0:T(8,128)S(1)}, u32[]{:S(2)}, u32[]{:S(2)}) %collective-permute-start.8) | collective-permute-done | bytes 69664 | tf_op jit(solution)/shard_map/while/body/eval_jaxpr/ppermute | solution.py:41
  52.7 2.8 %collective-permute-start.13 = (f32[32,512]{1,0:T(8,128)S(1)}, f32[32,512]{1,0:T(8,128)S(1)}, u32[]{:S(2)}, u32[]{:S(2)}) collective-permute-start(f32[32,512]{1,0:T(8,128)S(1)} %get-tuple-element.487), channel_id=1, source_target_pairs={{0,96},{16,176},{32,128},{48,208},{64,160},{80,240},{96,192},{112,... | collective-permute-start | bytes 196616 | tf_op jit(solution)/shard_map/while/body/eval_jaxpr/ppermute | solution.py:34
  60.7 3.2 %collective-permute-done.14 = f32[32,512]{1,0:T(8,128)S(1)} collective-permute-done((f32[32,512]{1,0:T(8,128)S(1)}, f32[32,512]{1,0:T(8,128)S(1)}, u32[]{:S(2)}, u32[]{:S(2)}) %collective-permute-start.14) | collective-permute-done | bytes 65568 | tf_op jit(solution)/shard_map/while/body/eval_jaxpr/ppermute | solution.py:34
  74.8 3.2 %collective-permute-done.2 = f32[136,128]{1,0:T(8,128)S(1)} collective-permute-done((f32[136,128]{1,0:T(8,128)S(1)}, f32[136,128]{1,0:T(8,128)S(1)}, u32[]{:S(2)}, u32[]{:S(2)}) %collective-permute-start.2) | collective-permute-done | bytes 69664 | tf_op jit(solution)/shard_map/while/body/eval_jaxpr/ppermute | solution.py:34
  78.0 5.3 %collective-permute-start.4 = (f32[544,128]{1,0:T(8,128)S(1)}, f32[544,128]{1,0:T(8,128)S(1)}, u32[]{:S(2)}, u32[]{:S(2)}) collective-permute-start(f32[544,128]{1,0:T(8,128)S(1)} %constant_dynamic-update-slice_fusion.15.mine), channel_id=1, source_target_pairs={{0,16},{16,0},{1,17},{17,1},{2,18},{18,2},{3,19},{19,3},{4,20},{20... | collective-permute-start | bytes 835592 | tf_op jit(solution)/shard_map/while/body/eval_jaxpr/ppermute | solution.py:25
  84.5 3.5 %eval_jaxpr.29 = (f32[136,128]{1,0:T(8,128)S(1)}, f32[8,32,512]{2,1,0:T(8,128)S(1)}, f32[32,512]{1,0:T(8,128)S(1)}) custom-call(s32[4]{0:T(128)S(1)} %pad_add_fusion.3.place, bf16[512,4096]{1,0:T(8,128)(2,1)S(1)} %copy-done, bf16[512,4096]{1,0:T(8,128)(2,1)S(1)} %copy-done.2, f32[32,512]{1,0:T(8,128)S(1)} %get-tuple-element.510.chip, ...), custom_call_target="tpu_custom_call" | custom-call | flops 1000000000 | bytes 8388608 | tf_op jit(solution)/shard_map/while/body/eval_jaxpr/pallas_call | solution.py:184
  107.5 2.8 %collective-permute-start.14 = (f32[32,512]{1,0:T(8,128)S(1)}, f32[32,512]{1,0:T(8,128)S(1)}, u32[]{:S(2)}, u32[]{:S(2)}) collective-permute-start(f32[32,512]{1,0:T(8,128)S(1)} %get-tuple-element.488), channel_id=1, source_target_pairs={{0,32},{16,240},{32,64},{48,16},{64,96},{80,48},{96,128},{112,80},... | collective-permute-start | bytes 196616 | tf_op jit(solution)/shard_map/while/body/eval_jaxpr/ppermute | solution.py:34
  111.0 3.7 %collective-permute-done.13 = f32[32,512]{1,0:T(8,128)S(1)} collective-permute-done((f32[32,512]{1,0:T(8,128)S(1)}, f32[32,512]{1,0:T(8,128)S(1)}, u32[]{:S(2)}, u32[]{:S(2)}) %collective-permute-start.13) | collective-permute-done | bytes 65568 | tf_op jit(solution)/shard_map/while/body/eval_jaxpr/ppermute | solution.py:34
  115.1 2.8 %collective-permute-done.15 = f32[32,512]{1,0:T(8,128)S(1)} collective-permute-done((f32[32,512]{1,0:T(8,128)S(1)}, f32[32,512]{1,0:T(8,128)S(1)}, u32[]{:S(2)}, u32[]{:S(2)}) %collective-permute-start.15) | collective-permute-done | bytes 65568 | tf_op jit(solution)/shard_map/while/body/eval_jaxpr/ppermute | solution.py:34
  122.8 2.8 %collective-permute-start.2 = (f32[136,128]{1,0:T(8,128)S(1)}, f32[136,128]{1,0:T(8,128)S(1)}, u32[]{:S(2)}, u32[]{:S(2)}) collective-permute-start(f32[136,128]{1,0:T(8,128)S(1)} %eval_jaxpr.28), channel_id=1, source_target_pairs={{0,96},{16,176},{32,128},{48,208},{64,160},{80,240},{96,192},{112,... | collective-permute-start | bytes 208904 | tf_op jit(solution)/shard_map/while/body/eval_jaxpr/ppermute | solution.py:34
  126.2 2.8 %collective-permute-done.1 = f32[136,128]{1,0:T(8,128)S(1)} collective-permute-done((f32[136,128]{1,0:T(8,128)S(1)}, f32[136,128]{1,0:T(8,128)S(1)}, u32[]{:S(2)}, u32[]{:S(2)}) %collective-permute-start.1) | collective-permute-done | bytes 69664 | tf_op jit(solution)/shard_map/while/body/eval_jaxpr/ppermute | solution.py:34
  131.0 3.3 %collective-permute-start.4 = (f32[544,128]{1,0:T(8,128)S(1)}, f32[544,128]{1,0:T(8,128)S(1)}, u32[]{:S(2)}, u32[]{:S(2)}) collective-permute-start(f32[544,128]{1,0:T(8,128)S(1)} %constant_dynamic-update-slice_fusion.15.mine), channel_id=1, source_target_pairs={{0,16},{16,0},{1,17},{17,1},{2,18},{18,2},{3,19},{19,3},{4,20},{20... | collective-permute-start | bytes 835592 | tf_op jit(solution)/shard_map/while/body/eval_jaxpr/ppermute | solution.py:25
  135.4 3.5 %eval_jaxpr.29 = (f32[136,128]{1,0:T(8,128)S(1)}, f32[8,32,512]{2,1,0:T(8,128)S(1)}, f32[32,512]{1,0:T(8,128)S(1)}) custom-call(s32[4]{0:T(128)S(1)} %pad_add_fusion.3.place, bf16[512,4096]{1,0:T(8,128)(2,1)S(1)} %copy-done, bf16[512,4096]{1,0:T(8,128)(2,1)S(1)} %copy-done.2, f32[32,512]{1,0:T(8,128)S(1)} %get-tuple-element.510.chip, ...), custom_call_target="tpu_custom_call" | custom-call | flops 1000000000 | bytes 8388608 | tf_op jit(solution)/shard_map/while/body/eval_jaxpr/pallas_call | solution.py:184
  144.7 2.9 %collective-permute-done.7 = f32[136,128]{1,0:T(8,128)S(1)} collective-permute-done((f32[136,128]{1,0:T(8,128)S(1)}, f32[136,128]{1,0:T(8,128)S(1)}, u32[]{:S(2)}, u32[]{:S(2)}) %collective-permute-start.7) | collective-permute-done | bytes 69664 | tf_op jit(solution)/shard_map/while/body/eval_jaxpr/ppermute | solution.py:41
  152.1 3.2 %collective-permute-done.8.b = f32[136,128]{1,0:T(8,128)S(1)} collective-permute-done((f32[136,128]{1,0:T(8,128)S(1)}, f32[136,128]{1,0:T(8,128)S(1)}, u32[]{:S(2)}, u32[]{:S(2)}) %collective-permute-start.8) | collective-permute-done | bytes 69664 | tf_op jit(solution)/shard_map/while/body/eval_jaxpr/ppermute | solution.py:41
  161.9 2.7 %collective-permute-start.14 = (f32[32,512]{1,0:T(8,128)S(1)}, f32[32,512]{1,0:T(8,128)S(1)}, u32[]{:S(2)}, u32[]{:S(2)}) collective-permute-start(f32[32,512]{1,0:T(8,128)S(1)} %get-tuple-element.488), channel_id=1, source_target_pairs={{0,32},{16,240},{32,64},{48,16},{64,96},{80,48},{96,128},{112,80},... | collective-permute-start | bytes 196616 | tf_op jit(solution)/shard_map/while/body/eval_jaxpr/ppermute | solution.py:34
  164.7 3.3 %collective-permute-done.13 = f32[32,512]{1,0:T(8,128)S(1)} collective-permute-done((f32[32,512]{1,0:T(8,128)S(1)}, f32[32,512]{1,0:T(8,128)S(1)}, u32[]{:S(2)}, u32[]{:S(2)}) %collective-permute-start.13) | collective-permute-done | bytes 65568 | tf_op jit(solution)/shard_map/while/body/eval_jaxpr/ppermute | solution.py:34
  168.9 2.9 %collective-permute-done.15 = f32[32,512]{1,0:T(8,128)S(1)} collective-permute-done((f32[32,512]{1,0:T(8,128)S(1)}, f32[32,512]{1,0:T(8,128)S(1)}, u32[]{:S(2)}, u32[]{:S(2)}) %collective-permute-start.15) | collective-permute-done | bytes 65568 | tf_op jit(solution)/shard_map/while/body/eval_jaxpr/ppermute | solution.py:34
  176.6 3.0 %collective-permute-start.21 = (f32[136,128]{1,0:T(8,128)S(1)}, f32[136,128]{1,0:T(8,128)S(1)}, u32[]{:S(2)}, u32[]{:S(2)}) collective-permute-start(f32[136,128]{1,0:T(8,128)S(1)} %shard_map.86), channel_id=1, source_target_pairs={{0,96},{16,176},{32,128},{48,208},{64,160},{80,240},{96,192},{112,... | collective-permute-start | bytes 208904 | tf_op jit(solution)/shard_map/ppermute | solution.py:34
  184.0 5.9 %collective-permute-start.23 = (f32[544,128]{1,0:T(8,128)S(1)}, f32[544,128]{1,0:T(8,128)S(1)}, u32[]{:S(2)}, u32[]{:S(2)}) collective-permute-start(f32[544,128]{1,0:T(8,128)S(1)} %constant_dynamic-update-slice_fusion.4.mine), channel_id=1, source_target_pairs={{0,16},{16,0},{1,17},{17,1},{2,18},{18,2},{3,19},{19,3},{4,20},{20... | collective-permute-start | bytes 835592 | tf_op jit(solution)/shard_map/ppermute | solution.py:25
  191.1 3.5 %shard_map.87 = (f32[136,128]{1,0:T(8,128)S(1)}, f32[8,32,512]{2,1,0:T(8,128)S(1)}, f32[32,512]{1,0:T(8,128)S(1)}) custom-call(s32[4]{0:T(128)S(1)} %pad_add_fusion.1.place, bf16[512,4096]{1,0:T(8,128)(2,1)S(1)} %copy-done.1, bf16[512,4096]{1,0:T(8,128)(2,1)S(1)} %copy-done.3, f32[32,512]{1,0:T(8,128)S(1)} %get-tuple-element.325.chip, ...), custom_call_target="tpu_custom_call" | custom-call | flops 1000000000 | bytes 8388608 | tf_op jit(solution)/shard_map/pallas_call | solution.py:184
  194.6 3.0 %collective-permute-start.24 = (f32[136,128]{1,0:T(8,128)S(1)}, f32[136,128]{1,0:T(8,128)S(1)}, u32[]{:S(2)}, u32[]{:S(2)}) collective-permute-start(f32[136,128]{1,0:T(8,128)S(1)} %get-tuple-element.332), channel_id=1, source_target_pairs={{0,2},{1,3},{2,0},{3,1},{4,6},{5,7},{6,4},{7,5},{8,10},{9,11},{10,... | collective-permute-start | bytes 208904 | tf_op jit(solution)/shard_map/ppermute | solution.py:41
  205.0 3.1 %collective-permute-start.29 = (f32[136,128]{1,0:T(8,128)S(1)}, f32[136,128]{1,0:T(8,128)S(1)}, u32[]{:S(2)}, u32[]{:S(2)}) collective-permute-start(f32[136,128]{1,0:T(8,128)S(1)} %add_add_fusion.2), channel_id=1, source_target_pairs={{0,12},{4,0},{8,4},{12,8},{1,13},{5,1},{9,5},{13,9},{2,14},{6,2},{... | collective-permute-start | bytes 208904 | tf_op jit(solution)/shard_map/ppermute | solution.py:41
  211.3 3.9 %all-to-all-start = ((f32[16,8,128]{2,1,0:T(8,128)}), f32[16,8,128]{2,1,0:T(8,128)S(1)}, u32[]{:S(2)}, u32[]{:S(2)}) async-start(f32[16,8,128]{2,1,0:T(8,128)} %broadcast_in_dim.22), calls=%async_computation | async-start | bytes 131072 | tf_op jit(solution)/shard_map/all_to_all | solution.py:307
  215.2 7.8 %all-to-all-done = f32[16,8,128]{2,1,0:T(8,128)S(1)} async-done(((f32[16,8,128]{2,1,0:T(8,128)}), f32[16,8,128]{2,1,0:T(8,128)S(1)}, u32[]{:S(2)}, u32[]{:S(2)}) %all-to-all-start) | async-done | bytes 65568 | tf_op jit(solution)/shard_map/all_to_all | solution.py:307
  (215 shorter events, 109.8 us)
Async XLA Ops:
  0.6 9.1 %collective-permute-start.17 = (f32[32,256]{1,0:T(8,128)}, f32[32,256]{1,0:T(8,128)S(1)}, u32[]{:S(2)}, u32[]{:S(2)}) collective-permute-start(f32[32,256]{1,0:T(8,128)} %param.10), channel_id=1, source_target_pairs={{0,16},{16,0},{1,17},{17,1},{2,18},{18,2},{3,19},{19,3},{4,20},{20... | collective-permute-start | bytes 98312 | tf_op jit(solution)/shard_map/ppermute | solution.py:25
  1.6 8.2 %collective-permute-start.18 = (f32[32,256]{1,0:T(8,128)S(1)}, f32[32,256]{1,0:T(8,128)S(1)}, u32[]{:S(2)}, u32[]{:S(2)}) collective-permute-start(f32[32,256]{1,0:T(8,128)S(1)} %subtract_multiply_fusion), channel_id=1, source_target_pairs={{0,16},{16,0},{1,17},{17,1},{2,18},{18,2},{3,19},{19,3},{4,20},{20... | collective-permute-start | bytes 98312 | tf_op jit(solution)/shard_map/ppermute | solution.py:25
  10.0 9.9 %collective-permute-start = (f32[136,128]{1,0:T(8,128)S(1)}, f32[136,128]{1,0:T(8,128)S(1)}, u32[]{:S(2)}, u32[]{:S(2)}) collective-permute-start(f32[136,128]{1,0:T(8,128)S(1)} %eval_jaxpr.28), channel_id=1, source_target_pairs={{0,32},{16,240},{32,64},{48,16},{64,96},{80,48},{96,128},{112,80},... | collective-permute-start | bytes 208904 | tf_op jit(solution)/shard_map/while/body/eval_jaxpr/ppermute | solution.py:34
  12.0 9.2 %collective-permute-start.1 = (f32[136,128]{1,0:T(8,128)S(1)}, f32[136,128]{1,0:T(8,128)S(1)}, u32[]{:S(2)}, u32[]{:S(2)}) collective-permute-start(f32[136,128]{1,0:T(8,128)S(1)} %eval_jaxpr.28), channel_id=1, source_target_pairs={{0,64},{16,208},{32,96},{48,240},{64,128},{80,16},{96,160},{112,48... | collective-permute-start | bytes 208904 | tf_op jit(solution)/shard_map/while/body/eval_jaxpr/ppermute | solution.py:34
  15.2 8.3 %collective-permute-start.2 = (f32[136,128]{1,0:T(8,128)S(1)}, f32[136,128]{1,0:T(8,128)S(1)}, u32[]{:S(2)}, u32[]{:S(2)}) collective-permute-start(f32[136,128]{1,0:T(8,128)S(1)} %eval_jaxpr.28), channel_id=1, source_target_pairs={{0,96},{16,176},{32,128},{48,208},{64,160},{80,240},{96,192},{112,... | collective-permute-start | bytes 208904 | tf_op jit(solution)/shard_map/while/body/eval_jaxpr/ppermute | solution.py:34
  33.3 5.9 %collective-permute-start.7 = (f32[136,128]{1,0:T(8,128)S(1)}, f32[136,128]{1,0:T(8,128)S(1)}, u32[]{:S(2)}, u32[]{:S(2)}) collective-permute-start(f32[136,128]{1,0:T(8,128)S(1)} %get-tuple-element.480), channel_id=1, source_target_pairs={{0,2},{1,3},{2,0},{3,1},{4,6},{5,7},{6,4},{7,5},{8,10},{9,11},{10,... | collective-permute-start | bytes 208904 | tf_op jit(solution)/shard_map/while/body/eval_jaxpr/ppermute | solution.py:41
  43.0 5.9 %collective-permute-start.9 = (f32[136,128]{1,0:T(8,128)S(1)}, f32[136,128]{1,0:T(8,128)S(1)}, u32[]{:S(2)}, u32[]{:S(2)}) collective-permute-start(f32[136,128]{1,0:T(8,128)S(1)} %add_add_fusion.4.a), channel_id=1, source_target_pairs={{0,4},{4,8},{8,12},{12,0},{1,5},{5,9},{9,13},{13,1},{2,6},{6,10},{... | collective-permute-start | bytes 208904 | tf_op jit(solution)/shard_map/while/body/eval_jaxpr/ppermute | solution.py:41
  52.0 6.3 %collective-permute-start.12 = (f32[32,512]{1,0:T(8,128)S(1)}, f32[32,512]{1,0:T(8,128)S(1)}, u32[]{:S(2)}, u32[]{:S(2)}) collective-permute-start(f32[32,512]{1,0:T(8,128)S(1)} %get-tuple-element.486), channel_id=1, source_target_pairs={{16,144},{48,176},{80,208},{112,240},{144,16},{176,48},{208,80},{2... | collective-permute-start | bytes 196616 | tf_op jit(solution)/shard_map/while/body/eval_jaxpr/ppermute | solution.py:34
  52.7 8.0 %collective-permute-start.13 = (f32[32,512]{1,0:T(8,128)S(1)}, f32[32,512]{1,0:T(8,128)S(1)}, u32[]{:S(2)}, u32[]{:S(2)}) collective-permute-start(f32[32,512]{1,0:T(8,128)S(1)} %get-tuple-element.487), channel_id=1, source_target_pairs={{0,96},{16,176},{32,128},{48,208},{64,160},{80,240},{96,192},{112,... | collective-permute-start | bytes 196616 | tf_op jit(solution)/shard_map/while/body/eval_jaxpr/ppermute | solution.py:34
  55.5 8.4 %collective-permute-start.14 = (f32[32,512]{1,0:T(8,128)S(1)}, f32[32,512]{1,0:T(8,128)S(1)}, u32[]{:S(2)}, u32[]{:S(2)}) collective-permute-start(f32[32,512]{1,0:T(8,128)S(1)} %get-tuple-element.488), channel_id=1, source_target_pairs={{0,32},{16,240},{32,64},{48,16},{64,96},{80,48},{96,128},{112,80},... | collective-permute-start | bytes 196616 | tf_op jit(solution)/shard_map/while/body/eval_jaxpr/ppermute | solution.py:34
  57.7 7.1 %collective-permute-start.15 = (f32[32,512]{1,0:T(8,128)S(1)}, f32[32,512]{1,0:T(8,128)S(1)}, u32[]{:S(2)}, u32[]{:S(2)}) collective-permute-start(f32[32,512]{1,0:T(8,128)S(1)} %get-tuple-element.489), channel_id=1, source_target_pairs={{0,64},{16,208},{32,96},{48,240},{64,128},{80,16},{96,160},{112,48... | collective-permute-start | bytes 196616 | tf_op jit(solution)/shard_map/while/body/eval_jaxpr/ppermute | solution.py:34
  68.3 6.4 %collective-permute-start.1 = (f32[136,128]{1,0:T(8,128)S(1)}, f32[136,128]{1,0:T(8,128)S(1)}, u32[]{:S(2)}, u32[]{:S(2)}) collective-permute-start(f32[136,128]{1,0:T(8,128)S(1)} %eval_jaxpr.28), channel_id=1, source_target_pairs={{0,64},{16,208},{32,96},{48,240},{64,128},{80,16},{96,160},{112,48... | collective-permute-start | bytes 208904 | tf_op jit(solution)/shard_map/while/body/eval_jaxpr/ppermute | solution.py:34
  70.4 7.5 %collective-permute-start.2 = (f32[136,128]{1,0:T(8,128)S(1)}, f32[136,128]{1,0:T(8,128)S(1)}, u32[]{:S(2)}, u32[]{:S(2)}) collective-permute-start(f32[136,128]{1,0:T(8,128)S(1)} %eval_jaxpr.28), channel_id=1, source_target_pairs={{0,96},{16,176},{32,128},{48,208},{64,160},{80,240},{96,192},{112,... | collective-permute-start | bytes 208904 | tf_op jit(solution)/shard_map/while/body/eval_jaxpr/ppermute | solution.py:34
  78.0 6.5 %collective-permute-start.4 = (f32[544,128]{1,0:T(8,128)S(1)}, f32[544,128]{1,0:T(8,128)S(1)}, u32[]{:S(2)}, u32[]{:S(2)}) collective-permute-start(f32[544,128]{1,0:T(8,128)S(1)} %constant_dynamic-update-slice_fusion.15.mine), channel_id=1, source_target_pairs={{0,16},{16,0},{1,17},{17,1},{2,18},{18,2},{3,19},{19,3},{4,20},{20... | collective-permute-start | bytes 835592 | tf_op jit(solution)/shard_map/while/body/eval_jaxpr/ppermute | solution.py:25
  90.1 5.8 %collective-permute-start.7 = (f32[136,128]{1,0:T(8,128)S(1)}, f32[136,128]{1,0:T(8,128)S(1)}, u32[]{:S(2)}, u32[]{:S(2)}) collective-permute-start(f32[136,128]{1,0:T(8,128)S(1)} %get-tuple-element.480), channel_id=1, source_target_pairs={{0,2},{1,3},{2,0},{3,1},{4,6},{5,7},{6,4},{7,5},{8,10},{9,11},{10,... | collective-permute-start | bytes 208904 | tf_op jit(solution)/shard_map/while/body/eval_jaxpr/ppermute | solution.py:41
  96.6 6.3 %collective-permute-start.8 = (f32[136,128]{1,0:T(8,128)S(1)}, f32[136,128]{1,0:T(8,128)S(1)}, u32[]{:S(2)}, u32[]{:S(2)}) collective-permute-start(f32[136,128]{1,0:T(8,128)S(1)} %add_add_fusion.4.a), channel_id=1, source_target_pairs={{0,8},{4,12},{8,0},{12,4},{1,9},{5,13},{9,1},{13,5},{2,10},{6,14},... | collective-permute-start | bytes 208904 | tf_op jit(solution)/shard_map/while/body/eval_jaxpr/ppermute | solution.py:41
  97.4 6.0 %collective-permute-start.9 = (f32[136,128]{1,0:T(8,128)S(1)}, f32[136,128]{1,0:T(8,128)S(1)}, u32[]{:S(2)}, u32[]{:S(2)}) collective-permute-start(f32[136,128]{1,0:T(8,128)S(1)} %add_add_fusion.4.a), channel_id=1, source_target_pairs={{0,4},{4,8},{8,12},{12,0},{1,5},{5,9},{9,13},{13,1},{2,6},{6,10},{... | collective-permute-start | bytes 208904 | tf_op jit(solution)/shard_map/while/body/eval_jaxpr/ppermute | solution.py:41
  107.2 7.5 %collective-permute-start.13 = (f32[32,512]{1,0:T(8,128)S(1)}, f32[32,512]{1,0:T(8,128)S(1)}, u32[]{:S(2)}, u32[]{:S(2)}) collective-permute-start(f32[32,512]{1,0:T(8,128)S(1)} %get-tuple-element.487), channel_id=1, source_target_pairs={{0,96},{16,176},{32,128},{48,208},{64,160},{80,240},{96,192},{112,... | collective-permute-start | bytes 196616 | tf_op jit(solution)/shard_map/while/body/eval_jaxpr/ppermute | solution.py:34
  107.5 7.6 %collective-permute-start.14 = (f32[32,512]{1,0:T(8,128)S(1)}, f32[32,512]{1,0:T(8,128)S(1)}, u32[]{:S(2)}, u32[]{:S(2)}) collective-permute-start(f32[32,512]{1,0:T(8,128)S(1)} %get-tuple-element.488), channel_id=1, source_target_pairs={{0,32},{16,240},{32,64},{48,16},{64,96},{80,48},{96,128},{112,80},... | collective-permute-start | bytes 196616 | tf_op jit(solution)/shard_map/while/body/eval_jaxpr/ppermute | solution.py:34
  110.3 7.6 %collective-permute-start.15 = (f32[32,512]{1,0:T(8,128)S(1)}, f32[32,512]{1,0:T(8,128)S(1)}, u32[]{:S(2)}, u32[]{:S(2)}) collective-permute-start(f32[32,512]{1,0:T(8,128)S(1)} %get-tuple-element.489), channel_id=1, source_target_pairs={{0,64},{16,208},{32,96},{48,240},{64,128},{80,16},{96,160},{112,48... | collective-permute-start | bytes 196616 | tf_op jit(solution)/shard_map/while/body/eval_jaxpr/ppermute | solution.py:34
  121.8 7.2 %collective-permute-start.1 = (f32[136,128]{1,0:T(8,128)S(1)}, f32[136,128]{1,0:T(8,128)S(1)}, u32[]{:S(2)}, u32[]{:S(2)}) collective-permute-start(f32[136,128]{1,0:T(8,128)S(1)} %eval_jaxpr.28), channel_id=1, source_target_pairs={{0,64},{16,208},{32,96},{48,240},{64,128},{80,16},{96,160},{112,48... | collective-permute-start | bytes 208904 | tf_op jit(solution)/shard_map/while/body/eval_jaxpr/ppermute | solution.py:34
  122.8 8.2 %collective-permute-start.2 = (f32[136,128]{1,0:T(8,128)S(1)}, f32[136,128]{1,0:T(8,128)S(1)}, u32[]{:S(2)}, u32[]{:S(2)}) collective-permute-start(f32[136,128]{1,0:T(8,128)S(1)} %eval_jaxpr.28), channel_id=1, source_target_pairs={{0,96},{16,176},{32,128},{48,208},{64,160},{80,240},{96,192},{112,... | collective-permute-start | bytes 208904 | tf_op jit(solution)/shard_map/while/body/eval_jaxpr/ppermute | solution.py:34
  141.6 5.9 %collective-permute-start.7 = (f32[136,128]{1,0:T(8,128)S(1)}, f32[136,128]{1,0:T(8,128)S(1)}, u32[]{:S(2)}, u32[]{:S(2)}) collective-permute-start(f32[136,128]{1,0:T(8,128)S(1)} %get-tuple-element.480), channel_id=1, source_target_pairs={{0,2},{1,3},{2,0},{3,1},{4,6},{5,7},{6,4},{7,5},{8,10},{9,11},{10,... | collective-permute-start | bytes 208904 | tf_op jit(solution)/shard_map/while/body/eval_jaxpr/ppermute | solution.py:41
  159.9 8.2 %collective-permute-start.13 = (f32[32,512]{1,0:T(8,128)S(1)}, f32[32,512]{1,0:T(8,128)S(1)}, u32[]{:S(2)}, u32[]{:S(2)}) collective-permute-start(f32[32,512]{1,0:T(8,128)S(1)} %get-tuple-element.487), channel_id=1, source_target_pairs={{0,96},{16,176},{32,128},{48,208},{64,160},{80,240},{96,192},{112,... | collective-permute-start | bytes 196616 | tf_op jit(solution)/shard_map/while/body/eval_jaxpr/ppermute | solution.py:34
  161.9 7.1 %collective-permute-start.14 = (f32[32,512]{1,0:T(8,128)S(1)}, f32[32,512]{1,0:T(8,128)S(1)}, u32[]{:S(2)}, u32[]{:S(2)}) collective-permute-start(f32[32,512]{1,0:T(8,128)S(1)} %get-tuple-element.488), channel_id=1, source_target_pairs={{0,32},{16,240},{32,64},{48,16},{64,96},{80,48},{96,128},{112,80},... | collective-permute-start | bytes 196616 | tf_op jit(solution)/shard_map/while/body/eval_jaxpr/ppermute | solution.py:34
  164.6 7.3 %collective-permute-start.15 = (f32[32,512]{1,0:T(8,128)S(1)}, f32[32,512]{1,0:T(8,128)S(1)}, u32[]{:S(2)}, u32[]{:S(2)}) collective-permute-start(f32[32,512]{1,0:T(8,128)S(1)} %get-tuple-element.489), channel_id=1, source_target_pairs={{0,64},{16,208},{32,96},{48,240},{64,128},{80,16},{96,160},{112,48... | collective-permute-start | bytes 196616 | tf_op jit(solution)/shard_map/while/body/eval_jaxpr/ppermute | solution.py:34
  175.0 6.4 %collective-permute-start.20 = (f32[136,128]{1,0:T(8,128)S(1)}, f32[136,128]{1,0:T(8,128)S(1)}, u32[]{:S(2)}, u32[]{:S(2)}) collective-permute-start(f32[136,128]{1,0:T(8,128)S(1)} %shard_map.86), channel_id=1, source_target_pairs={{0,64},{16,208},{32,96},{48,240},{64,128},{80,16},{96,160},{112,48... | collective-permute-start | bytes 208904 | tf_op jit(solution)/shard_map/ppermute | solution.py:34
  176.6 7.4 %collective-permute-start.21 = (f32[136,128]{1,0:T(8,128)S(1)}, f32[136,128]{1,0:T(8,128)S(1)}, u32[]{:S(2)}, u32[]{:S(2)}) collective-permute-start(f32[136,128]{1,0:T(8,128)S(1)} %shard_map.86), channel_id=1, source_target_pairs={{0,96},{16,176},{32,128},{48,208},{64,160},{80,240},{96,192},{112,... | collective-permute-start | bytes 208904 | tf_op jit(solution)/shard_map/ppermute | solution.py:34
  184.0 7.1 %collective-permute-start.23 = (f32[544,128]{1,0:T(8,128)S(1)}, f32[544,128]{1,0:T(8,128)S(1)}, u32[]{:S(2)}, u32[]{:S(2)}) collective-permute-start(f32[544,128]{1,0:T(8,128)S(1)} %constant_dynamic-update-slice_fusion.4.mine), channel_id=1, source_target_pairs={{0,16},{16,0},{1,17},{17,1},{2,18},{18,2},{3,19},{19,3},{4,20},{20... | collective-permute-start | bytes 835592 | tf_op jit(solution)/shard_map/ppermute | solution.py:25
  194.6 6.0 %collective-permute-start.24 = (f32[136,128]{1,0:T(8,128)S(1)}, f32[136,128]{1,0:T(8,128)S(1)}, u32[]{:S(2)}, u32[]{:S(2)}) collective-permute-start(f32[136,128]{1,0:T(8,128)S(1)} %get-tuple-element.332), channel_id=1, source_target_pairs={{0,2},{1,3},{2,0},{3,1},{4,6},{5,7},{6,4},{7,5},{8,10},{9,11},{10,... | collective-permute-start | bytes 208904 | tf_op jit(solution)/shard_map/ppermute | solution.py:41
  203.5 5.9 %collective-permute-start.27 = (f32[136,128]{1,0:T(8,128)S(1)}, f32[136,128]{1,0:T(8,128)S(1)}, u32[]{:S(2)}, u32[]{:S(2)}) collective-permute-start(f32[136,128]{1,0:T(8,128)S(1)} %add_add_fusion.2), channel_id=1, source_target_pairs={{0,8},{4,12},{8,0},{12,4},{1,9},{5,13},{9,1},{13,5},{2,10},{6,14},... | collective-permute-start | bytes 208904 | tf_op jit(solution)/shard_map/ppermute | solution.py:41
  211.3 11.7 %all-to-all-start = ((f32[16,8,128]{2,1,0:T(8,128)}), f32[16,8,128]{2,1,0:T(8,128)S(1)}, u32[]{:S(2)}, u32[]{:S(2)}) async-start(f32[16,8,128]{2,1,0:T(8,128)} %broadcast_in_dim.22), calls=%async_computation | async-start | bytes 131072 | tf_op jit(solution)/shard_map/all_to_all | solution.py:307
  (45 other events, 335.9 us)
